TPU v7x, 32 devices: a whole 2x2x4 slice. The times are simulated.
32 devices in a mesh: lat: 4 (over x, core), lon: 8 (over z, y).
Axes of the slice: x: 2, y: 2, z: 4, core: 2. Of those that a mesh axis runs over, the one named last changes fastest.
Arguments:
- nodes: bfloat16 [4, 8, 384, 512], P('lat', 'lon'), may hold values from -6 to 6
- edges: bfloat16 [4, 8, 3072, 512], P('lat', 'lon'), may hold values from -6 to 6
- senders: int32 [4, 8, 3072], P('lat', 'lon'), may hold values from 0 to 511, as said below
- receivers: int32 [4, 8, 3072], P('lat', 'lon'), may hold values from 0 to 383
- edge_count: int32 [4, 8], P('lat', 'lon'), may hold values from 1536 to 3072, as said below
- halo_send: int32 [4, 8, 4, 24], P('lat', 'lon'), may hold values from 0 to 383
- long_need: int32 [4, 8, 32, 1], P('lat', 'lon'), may hold values from 0 to 1
- node_cot: bfloat16 [4, 8, 384, 512], P('lat', 'lon'), may hold values from -6 to 6
- edge_cot: bfloat16 [4, 8, 3072, 512], P('lat', 'lon'), may hold values from -6 to 6
- e_w1: bfloat16 [1536, 512], replicated, may hold values from -0.15625 to 0.15625
- e_b1: float32 [512], replicated, may hold values from -3 to 3
- e_w2: bfloat16 [512, 512], replicated, may hold values from -0.25 to 0.25
- e_gain: float32 [512], replicated, may hold values from 0.25 to 1.75
- n_w1: bfloat16 [1024, 512], replicated, may hold values from -0.1875 to 0.1875
- n_b1: float32 [512], replicated, may hold values from -3 to 3
- n_w2: bfloat16 [512, 512], replicated, may hold values from -0.25 to 0.25
- n_gain: float32 [512], replicated, may hold values from 0.25 to 1.75
Outputs:
- new_nodes: bfloat16 [4, 8, 384, 512], P('lat', 'lon')
- new_edges: bfloat16 [4, 8, 3072, 512], P('lat', 'lon')
- node_grad: float32 [4, 8, 384, 512], P('lat', 'lon')
- edge_grad: float32 [4, 8, 3072, 512], P('lat', 'lon')
- e_w1_grad: float32 [1536, 512], P(('lat', 'lon'))
- e_b1_grad: float32 [512], P(('lat', 'lon'))
- e_w2_grad: float32 [512, 512], P(('lat', 'lon'))
- e_gain_grad: float32 [512], P(('lat', 'lon'))
- n_w1_grad: float32 [1024, 512], P(('lat', 'lon'))
- n_b1_grad: float32 [512], P(('lat', 'lon'))
- n_w2_grad: float32 [512, 512], P(('lat', 'lon'))
- n_gain_grad: float32 [512], P(('lat', 'lon'))
Inputs may be any that keep to these rules, and one draw needn't show every extreme that they name: `senders`: entries below 384 are a region's own nodes, the next 96 the four neighbour blocks, the rest the coarse rows; the third block is never named in the first band and the fourth never in the last. The first three edge slots of region r name the coarse rows of regions r + 1, r - 1 and r + 16 in flat order, counted round. `edge_count`: some region has all 3072 slots live. `long_need`: A region's coarse nodes are its first 2 rows.
All inputs are finite; a program needn't handle non-finite values.
Results may differ from a plain program's by a relative error of at most 0.009.
Values may be sent and summed in bfloat16 or wider, within the bound.
A program may use at most 192 MiB of HBM per device.

v0:
```python
import jax
import jax.numpy as jnp
from jax import lax
from jax.sharding import PartitionSpec as P

COARSE = 2


EPS = 1e-05


def shifted(block, axis, distance):
    devices = range(lax.axis_size(axis))
    route = [((i - distance) % len(devices), i) for i in devices]
    return lax.ppermute(block, axis, route)


def passed_along(value, axis, steps):
    count = lax.axis_size(axis)
    leading, last = (max(0, -steps), min(count, count - steps))
    return lax.ppermute(value, axis, [(source, source + steps) for source in range(leading, last)])


def layer_norm(z, gain):
    mean = jnp.mean(z, axis=-1, keepdims=True)
    centred = z - mean
    rstd = lax.rsqrt(jnp.mean(centred * centred, axis=-1, keepdims=True) + EPS)
    normed = centred * rstd
    return (normed * gain, normed, rstd)


def transposed(left, right):
    return lax.dot_general(
        left, right, (((0,), (0,)), ((), ())), preferred_element_type=jnp.float32
    )


def mlp_forward(parts, w_first, b_first, w_second, gain):
    width = parts[0].shape[1]
    z_first = b_first
    for number, piece in enumerate(parts):
        z_first = z_first + jnp.dot(
            piece,
            w_first[number * width : (number + 1) * width],
            preferred_element_type=jnp.float32,
        )
    active = jax.nn.silu(z_first).astype(jnp.bfloat16)
    z_second = jnp.dot(active, w_second, preferred_element_type=jnp.float32)
    result, normed, rstd = layer_norm(z_second, gain)
    return (result, (z_first, active, normed, rstd))


def mlp_backward(parts, saved, grad_out, w_first, w_second, gain):
    z_first, active, normed, rstd = saved
    gain_grad = jnp.sum(grad_out * normed, axis=0)
    scaled = grad_out * gain
    g_second = rstd * (
        scaled
        - jnp.mean(scaled, axis=-1, keepdims=True)
        - normed * jnp.mean(scaled * normed, axis=-1, keepdims=True)
    )
    g_second = g_second.astype(jnp.bfloat16)
    second_grad = transposed(active, g_second)
    g_active = jnp.dot(g_second, w_second.T, preferred_element_type=jnp.float32)
    sigma = jax.nn.sigmoid(z_first)
    g_first = (g_active * sigma * (1.0 + z_first * (1.0 - sigma))).astype(jnp.bfloat16)
    bias_grad = jnp.sum(g_first, axis=0, dtype=jnp.float32)
    first_grad = jnp.concatenate([transposed(piece, g_first) for piece in parts], axis=0)
    g_input = jnp.dot(g_first, w_first.T, preferred_element_type=jnp.float32)
    return (g_input, (first_grad, bias_grad, second_grad, gain_grad))


def shards(
    nodes,
    edges,
    senders,
    receivers,
    edge_count,
    halo_send,
    long_need,
    node_cot,
    edge_cot,
    e_w1,
    e_b1,
    e_w2,
    e_gain,
    n_w1,
    n_b1,
    n_w2,
    n_gain,
):
    nodes_l = nodes[0, 0]
    edges_l = edges[0, 0]
    snd = senders[0, 0]
    rcv = receivers[0, 0]
    count = edge_count[0, 0]
    rows_out = halo_send[0, 0]
    need = long_need[0, 0]
    node_n, width = nodes_l.shape
    halo_n = rows_out.shape[1]
    devices, slot_n = need.shape
    axes = ("lat", "lon")

    def exchange(value):
        return lax.all_to_all(value, axes, split_axis=0, concat_axis=0, tiled=True)

    def one_hot(ids, count, keep=None):
        hit = ids[:, None] == jnp.arange(count)[None, :]
        if keep is not None:
            hit = hit & keep[:, None]
        return hit.astype(jnp.bfloat16)

    def one_hot_t(ids, count, keep=None):
        hit = ids[None, :] == jnp.arange(count)[:, None]
        if keep is not None:
            hit = hit & keep[None, :]
        return hit.astype(jnp.bfloat16)

    def product(left, right):
        return jnp.dot(left, right, preferred_element_type=jnp.float32)

    sent = product(one_hot(rows_out.reshape(-1), node_n), nodes_l).astype(jnp.bfloat16)
    sent = sent.reshape(4, halo_n, width)
    from_east = shifted(sent[0], "lon", 1)
    from_west = shifted(sent[1], "lon", -1)
    from_north = passed_along(sent[2], "lat", 1)
    from_south = passed_along(sent[3], "lat", -1)
    coarse = exchange(jnp.broadcast_to(nodes_l[:COARSE][None], (devices, COARSE, width)))
    far = jnp.zeros((devices, slot_n, width), jnp.bfloat16)
    for c in range(COARSE):
        far = jnp.where((need == c)[:, :, None], coarse[:, c][:, None, :], far)
    far = far.reshape(devices * slot_n, width)
    table = jnp.concatenate([nodes_l, from_east, from_west, from_north, from_south, far], axis=0)
    table_n = table.shape[0]
    w_edge, w_send, w_recv = (e_w1[i * width : (i + 1) * width] for i in range(3))
    alive = jnp.arange(edges_l.shape[0]) < count
    live = alive.astype(jnp.float32)[:, None]
    z_edge = product(edges_l, w_edge) + e_b1
    p_recv = product(nodes_l, w_recv).astype(jnp.bfloat16)
    p_send = product(table, w_send).astype(jnp.bfloat16)
    picked = jnp.concatenate([p_send, p_recv], axis=0)
    columns = jnp.arange(table_n + node_n)[None, :]
    pick = (
        ((snd[:, None] == columns) | (rcv[:, None] + table_n == columns)) & alive[:, None]
    ).astype(jnp.bfloat16)
    z_first = z_edge + product(pick, picked)
    active = jax.nn.silu(z_first).astype(jnp.bfloat16)
    z_second = product(active, e_w2)
    edge_out, normed, rstd = layer_norm(z_second, e_gain)
    new_edges = (edges_l + live * edge_out).astype(jnp.bfloat16)
    recv_t = one_hot_t(rcv, node_n, alive)
    aggregate = product(recv_t, new_edges).astype(jnp.bfloat16)
    node_parts = (nodes_l, aggregate)
    node_out, node_saved = mlp_forward(node_parts, n_w1, n_b1, n_w2, n_gain)
    new_nodes = (nodes_l + node_out).astype(jnp.bfloat16)
    node_up = node_cot[0, 0].astype(jnp.float32)
    g_node_in, node_grads = mlp_backward(node_parts, node_saved, node_up, n_w1, n_w2, n_gain)
    n_first, n_bias, n_second, n_scale = node_grads
    g_aggregate = g_node_in[:, width:].astype(jnp.bfloat16)
    g_new_edges = edge_cot[0, 0].astype(jnp.float32) + product(
        one_hot(rcv, node_n, alive), g_aggregate
    )
    grad_out = live * g_new_edges
    e_scale = jnp.sum(grad_out * normed, axis=0)
    scaled = grad_out * e_gain
    g_second = rstd * (
        scaled
        - jnp.mean(scaled, axis=-1, keepdims=True)
        - normed * jnp.mean(scaled * normed, axis=-1, keepdims=True)
    )
    g_second = g_second.astype(jnp.bfloat16)
    e_second = transposed(active, g_second)

    def split(value):
        return value.astype(jnp.bfloat16).reshape(devices, -1, value.shape[-1])

    early = exchange(jnp.concatenate([split(n_first), split(n_second), split(e_second)], axis=1))
    g_active = product(g_second, e_w2.T)
    sigma = jax.nn.sigmoid(z_first)
    g_first = (g_active * sigma * (1.0 + z_first * (1.0 - sigma))).astype(jnp.bfloat16)
    e_bias = jnp.sum(g_first, axis=0, dtype=jnp.float32)
    rows = jnp.arange(table_n + node_n)[:, None]
    pick_t = (
        ((snd[None, :] == rows) | (rcv[None, :] + table_n == rows)) & alive[None, :]
    ).astype(jnp.bfloat16)
    spread = product(pick_t, g_first).astype(jnp.bfloat16)
    spread_send, spread_recv = spread[:table_n], spread[table_n:]
    e_first = jnp.concatenate(
        [
            transposed(edges_l, g_first),
            transposed(table, spread_send),
            transposed(nodes_l, spread_recv),
        ],
        axis=0,
    )
    late = exchange(split(e_first))
    sender_grad = product(spread_send, w_send.T)
    edge_grad = g_new_edges + product(g_first, w_edge.T)
    halo_part = sender_grad[node_n : node_n + 4 * halo_n].astype(jnp.bfloat16)
    to_east = shifted(halo_part[:halo_n], "lon", -1)
    to_west = shifted(halo_part[halo_n : 2 * halo_n], "lon", 1)
    to_north = passed_along(halo_part[2 * halo_n : 3 * halo_n], "lat", -1)
    to_south = passed_along(halo_part[3 * halo_n :], "lat", 1)
    far_grad = sender_grad[node_n + 4 * halo_n :].reshape(devices, slot_n, width)
    to_coarse = jnp.stack(
        [
            jnp.sum(jnp.where((need == c)[:, :, None], far_grad, 0.0), axis=1)
            for c in range(COARSE)
        ],
        axis=1,
    ).astype(jnp.bfloat16)
    vectors = jnp.concatenate(
        [v.reshape(devices, -1) for v in (e_bias, e_scale, n_bias, n_scale)], axis=1
    )
    high = vectors.astype(jnp.bfloat16)
    low = (vectors - high.astype(jnp.float32)).astype(jnp.bfloat16)
    extra = jnp.concatenate([high, low], axis=1)
    vector_n = vectors.shape[1]
    extra_rows = -(-extra.shape[1] // width)
    extra = jnp.pad(extra, ((0, 0), (0, extra_rows * width - extra.shape[1])))
    came = exchange(
        jnp.concatenate([to_coarse, extra.reshape(devices, extra_rows, width)], axis=1)
    ).astype(jnp.float32)
    came = jnp.sum(came, axis=0)
    coarse_grad = came[:COARSE]
    flat = came[COARSE:].reshape(-1)
    vector = (flat[:vector_n] + flat[vector_n : 2 * vector_n]).reshape(4, -1)
    returned = jnp.concatenate([to_east, to_west, to_north, to_south], axis=0)
    border_t = one_hot_t(rows_out.reshape(-1), node_n)
    node_grad = (
        node_up
        + g_node_in[:, :width]
        + product(spread_recv, w_recv.T)
        + sender_grad[:node_n]
        + product(border_t, returned)
    )
    node_grad = node_grad + jnp.pad(coarse_grad, ((0, node_n - COARSE), (0, 0)))
    early = jnp.sum(early.astype(jnp.float32), axis=0)
    late = jnp.sum(late.astype(jnp.float32), axis=0)
    n_one = n_first.shape[0] // devices
    n_two = n_one + n_second.shape[0] // devices
    sums = (
        late,
        vector[0],
        early[n_two:],
        vector[1],
        early[:n_one],
        vector[2],
        early[n_one:n_two],
        vector[3],
    )
    return (
        new_nodes[None, None],
        new_edges[None, None],
        node_grad[None, None],
        edge_grad[None, None],
        sums[0],
        sums[1],
        sums[2],
        sums[3],
        sums[4],
        sums[5],
        sums[6],
        sums[7],
    )


def solution(mesh):
    return jax.shard_map(
        shards,
        mesh=mesh,
        in_specs=(
            P("lat", "lon", None, None),
            P("lat", "lon", None, None),
            P("lat", "lon", None),
            P("lat", "lon", None),
            P("lat", "lon"),
            P("lat", "lon", None, None),
            P("lat", "lon", None, None),
            P("lat", "lon", None, None),
            P("lat", "lon", None, None),
            P(),
            P(),
            P(),
            P(),
            P(),
            P(),
            P(),
            P(),
        ),
        out_specs=(
            P("lat", "lon", None, None),
            P("lat", "lon", None, None),
            P("lat", "lon", None, None),
            P("lat", "lon", None, None),
            P(("lat", "lon"), None),
            P(("lat", "lon")),
            P(("lat", "lon"), None),
            P(("lat", "lon")),
            P(("lat", "lon"), None),
            P(("lat", "lon")),
            P(("lat", "lon"), None),
            P(("lat", "lon")),
        ),
        check_vma=False,
    )
```

profile of v0, /device:TPU:0, one launch (start us, length us, event | category | flops | bytes accessed | tf_op | source)
XLA Modules:
  0.0 192.5 jit_solution(3141281326137853703)
XLA Ops:
  2.2 7.3 %all-to-all-start = ((bf16[32,2,512]{2,1,0:T(2,128)(2,1)}), bf16[32,2,512]{2,1,0:T(2,128)(2,1)S(1)}, u32[]{:S(2)}, u32[]{:S(2)}) async-start(bf16[32,2,512]{2,1,0:T(2,128)(2,1)} %broadcast_in_dim.47), calls=%async_computation | async-start | bytes 131072 | tf_op jit(solution)/shard_map/all_to_all | solution.py:105
  10.3 1.2 convolution_convert_fusion.8
  11.6 1.3 collective-permute-start.3
  12.9 3.0 %collective-permute-start.2 = (bf16[24,512]{1,0:T(8,128)(2,1)S(1)}, bf16[24,512]{1,0:T(8,128)(2,1)S(1)}, u32[]{:S(2)}, u32[]{:S(2)}) collective-permute-start(bf16[24,512]{1,0:T(8,128)(2,1)S(1)} %get-tuple-element.67), channel_id=1, source_target_pairs={{0,8},{8,16},{16,24},{1,9},{9,17},{17,25},{2,10},{10,18},{18,26},{... | collective-permute-start | bytes 73736 | tf_op jit(solution)/shard_map/ppermute | solution.py:21
  15.9 4.6 %collective-permute-start.1 = (bf16[24,512]{1,0:T(8,128)(2,1)S(1)}, bf16[24,512]{1,0:T(8,128)(2,1)S(1)}, u32[]{:S(2)}, u32[]{:S(2)}) collective-permute-start(bf16[24,512]{1,0:T(8,128)(2,1)S(1)} %get-tuple-element.68), channel_id=1, source_target_pairs={{1,0},{2,1},{3,2},{4,3},{5,4},{6,5},{7,6},{0,7},{9,8},{10,9},{11,1... | collective-permute-start | bytes 73736 | tf_op jit(solution)/shard_map/ppermute | solution.py:15
  20.5 1.0 bitcast_dynamic-update-slice_fusion
  23.6 2.3 %convolution_convert_fusion.7 = bf16[384,512]{1,0:T(8,128)(2,1)} fusion(bf16[1536,512]{1,0:T(8,128)(2,1)} %param.26, bf16[1,1,384,512]{3,2,1,0:T(8,128)(2,1)} %param.17), kind=kOutput, calls=%fused_computation.67 | convolution fusion | flops 201523200 | bytes 1310720 | tf_op jit(solution)/shard_map/dot_general | solution.py:120
  26.3 4.6 %copy.42 = bf16[1,1,3072,512]{2,3,1,0:T(8,128)(2,1)} copy(bf16[1,1,3072,512]{3,2,1,0:T(8,128)(2,1)} %param.25) | data formatting | bytes 6291456 | tf_op args[8]
  30.9 4.6 %copy.39 = bf16[1,1,3072,512]{2,3,1,0:T(8,128)(2,1)} copy(bf16[1,1,3072,512]{3,2,1,0:T(8,128)(2,1)} %param.18) | data formatting | bytes 6291456 | tf_op args[1]
  36.6 1.7 convolution_convert_fusion.6
  38.3 5.4 %fusion.2 = f32[3072,512]{1,0:T(8,128)S(1)} fusion(s32[3072]{0:T(1024)S(1)} %broadcast_add_fusion, s32[3072]{0:T(1024)} %bitcast.112, pred[3072]{0:T(1024)(128)(4,1)S(1)} %get-tuple-element.91, bf16[384,512]{1,0:T(8,128)(2,1)} %convolution_convert_fusion.7, bf16[512,512]{1,0:T(8,128)(2,1)S(1)} %convolution_convert_fusion.6), kind=kOutput, calls=%fused_computation.6 | convolution fusion | flops 2831417344 | bytes 7236608 | tf_op jit(solution)/shard_map/dot_general | solution.py:120
  43.7 4.0 %multiply_convert_fusion.2 = (bf16[3072,512]{1,0:T(8,128)(2,1)S(1)}, f32[3072,512]{1,0:T(8,128)}) fusion(f32[3072,512]{1,0:T(8,128)S(1)} %fusion.2, f32[512]{0:T(512)S(1)} %copy-done.42, bf16[1536,512]{1,0:T(8,128)(2,1)S(1)} %copy-done.20, bf16[1,1,3072,512]{3,2,1,0:T(8,128)(2,1)S(1)} %copy-done.17), kind=kOutput, calls=%fused_computation.19 | convolution fusion | flops 1621622784 | bytes 19400704 | tf_op jit(solution)/shard_map/dot_general | solution.py:120
  47.8 1.9 %fusion.102 = (f32[3072]{0:T(1024)S(1)}, f32[3072,512]{0,1:T(8,128)S(1)}) fusion(bf16[3072,512]{1,0:T(8,128)(2,1)S(1)} %get-tuple-element.78, bf16[512,512]{1,0:T(8,128)(2,1)S(1)} %copy-done), kind=kOutput, calls=%fused_computation.172 | convolution fusion | flops 1612182528 | bytes 9973760 | tf_op jit(solution)/shard_map/dot_general | solution.py:120
  50.6 1.1 copy-done.5
  51.6 1.8 add_convert_fusion
  53.4 1.4 fusion.38
  57.3 1.1 fusion.54
  60.4 4.3 %multiply_reduce_fusion = (f32[512]{0:T(512)S(1)}, f32[3072]{0:T(1024)S(1)}, f32[3072]{0:T(1024)S(1)}, f32[3072,512]{0,1:T(8,128)S(1)}) fusion(f32[3072,512]{0,1:T(8,128)S(1)} %get-tuple-element.81, f32[3072]{0:T(1024)S(1)} %add_rsqrt_fusion, f32[3072]{0:T(1024)S(1)} %broadcast_multiply_fusion.2, f32[3072]{0:T(1024)S(1)} %get-tuple-element.92, ...), kind=kOutput, calls=%fused_computation.12 | convolution fusion | flops 1227613696 | bytes 16202752 | tf_op jit(solution)/shard_map/dot_general | solution.py:120
  64.8 2.1 %multiply_convert_fusion.1 = bf16[3072,512]{0,1:T(8,128)(2,1)S(1)} fusion(f32[3072,512]{0,1:T(8,128)S(1)} %get-tuple-element.84, f32[3072,512]{0,1:T(8,128)S(1)} %get-tuple-element.81, f32[3072]{0:T(1024)S(1)} %broadcast_multiply_fusion, f32[3072]{0:T(1024)S(1)} %broadcast_multiply_fusion.1, f32[512]{0:T(512)S(1)} %copy-done.29, f32[3072]{0:T(1024)S(1)} %add_rsqrt_fusion, ...), kind=kLoop, calls=%fused_computation.15 | loop fusion | flops 14155776 | bytes 15792128 | tf_op jit(solution)/shard_map/convert_element_type | solution.py:171
  67.4 4.3 %convert_reduce_fusion = (f32[512]{0:T(512)S(1)}, bf16[3072,512]{1,0:T(8,128)(2,1)S(1)}) fusion(f32[3072,512]{1,0:T(8,128)S(1)} %bitcast.115, bf16[3072,512]{0,1:T(8,128)(2,1)S(1)} %multiply_convert_fusion.1, bf16[512,512]{1,0:T(8,128)(2,1)S(1)} %copy-done), kind=kOutput, calls=%fused_computation.13 | convolution fusion | flops 1627913728 | bytes 13109248 | tf_op jit(solution)/shard_map/dot_general | solution.py:120
  71.8 1.8 fusion.41
  73.7 3.0 %fusion.27 = bf16[896,512]{1,0:T(8,128)(2,1)S(1)} fusion(bf16[3072,512]{1,0:T(8,128)(2,1)S(1)} %get-tuple-element.88, s32[3072]{0:T(1024)S(1)} %broadcast_add_fusion, s32[3072]{0:T(1024)S(1)} %bitcast.113, pred[3072]{0:T(1024)(128)(4,1)S(1)} %copy-done.34), kind=kOutput, calls=%fused_computation.47 | convolution fusion | flops 2830041088 | bytes 4090880 | tf_op jit(solution)/shard_map/dot_general | solution.py:120
  76.7 1.3 convolution_convert_fusion.5
  78.5 1.3 fusion.104
  81.2 6.0 %all-to-all-start.1 = ((bf16[32,3,512]{2,1,0:T(4,128)(2,1)}), bf16[32,3,512]{2,1,0:T(4,128)(2,1)S(1)}, u32[]{:S(2)}, u32[]{:S(2)}) async-start(bf16[32,3,512]{2,1,0:T(4,128)(2,1)} %copy.43), calls=%async_computation.1 | async-start | bytes 262144 | tf_op jit(solution)/shard_map/all_to_all | solution.py:105
  87.2 2.3 %pad_maximum_fusion.1 = bf16[1536,512]{1,0:T(8,128)(2,1)} fusion(bf16[512,512]{1,0:T(8,128)(2,1)S(1)} %fusion.44, bf16[512,512]{1,0:T(8,128)(2,1)} %convolution_convert_fusion.5, bf16[512,512]{1,0:T(8,128)(2,1)S(1)} %fusion.41), kind=kLoop, calls=%fused_computation.46 | loop fusion | flops 4718592 | bytes 3145728 | tf_op jit(solution)/shard_map/concatenate | solution.py:188
  89.5 5.5 %all-to-all-done.1 = bf16[32,3,512]{2,1,0:T(4,128)(2,1)S(1)} async-done(((bf16[32,3,512]{2,1,0:T(4,128)(2,1)}), bf16[32,3,512]{2,1,0:T(4,128)(2,1)S(1)}, u32[]{:S(2)}, u32[]{:S(2)}) %all-to-all-start.1) | async-done | bytes 98336 | tf_op jit(solution)/shard_map/all_to_all | solution.py:105
  95.0 2.9 %all-to-all-start.2 = ((bf16[32,48,512]{2,1,0:T(8,128)(2,1)}), bf16[32,48,512]{2,1,0:T(8,128)(2,1)S(1)}, u32[]{:S(2)}, u32[]{:S(2)}) async-start(bf16[32,48,512]{2,1,0:T(8,128)(2,1)} %bitcast.105), calls=%async_computation.2 | async-start | bytes 3145728 | tf_op jit(solution)/shard_map/all_to_all | solution.py:105
  98.0 1.5 convolution_convert_fusion.2
  100.6 1.3 copy-done.8
  101.9 1.0 copy-done.16
  102.8 1.9 convolution_convert_fusion
  104.7 1.5 pad_maximum_fusion
  106.3 30.2 %all-to-all-done.2 = bf16[32,48,512]{2,1,0:T(8,128)(2,1)S(1)} async-done(((bf16[32,48,512]{2,1,0:T(8,128)(2,1)}), bf16[32,48,512]{2,1,0:T(8,128)(2,1)S(1)}, u32[]{:S(2)}, u32[]{:S(2)}) %all-to-all-start.2) | async-done | bytes 1572896 | tf_op jit(solution)/shard_map/all_to_all | solution.py:105
  136.5 1.2 copy-done.9
  137.6 2.7 %all-to-all-start.3 = ((bf16[32,64,512]{2,1,0:T(8,128)(2,1)}), bf16[32,64,512]{2,1,0:T(8,128)(2,1)S(1)}, u32[]{:S(2)}, u32[]{:S(2)}) async-start(bf16[32,64,512]{2,1,0:T(8,128)(2,1)} %pad_maximum_fusion), calls=%async_computation.3 | async-start | bytes 4194304 | tf_op jit(solution)/shard_map/all_to_all | solution.py:105
  140.4 4.6 %copy.45 = bf16[1,1,3072,512]{3,2,1,0:T(8,128)(2,1)} copy(bf16[1,1,3072,512]{2,3,1,0:T(8,128)(2,1)} %bitcast.104) | data formatting | bytes 6291456
  145.0 8.4 %add_bitcast_fusion = f32[1,1,3072,512]{2,3,1,0:T(8,128)} fusion(f32[3072,512]{0,1:T(8,128)} %copy-done.2, bf16[3072,512]{1,0:T(8,128)(2,1)} %copy-done.6, bf16[1536,512]{1,0:T(8,128)(2,1)} %param.26), kind=kOutput, calls=%fused_computation.11 | convolution fusion | flops 1612185600 | bytes 16252928 | tf_op jit(solution)/shard_map/dot_general | solution.py:120
  153.4 6.6 %copy.46 = f32[1,1,3072,512]{3,2,1,0:T(8,128)} copy(f32[1,1,3072,512]{2,3,1,0:T(8,128)} %add_bitcast_fusion) | data formatting | bytes 12582912
  160.0 0.9 fusion.98
  160.9 4.6 %collective-permute-start.4 = (bf16[24,512]{1,0:T(8,128)(2,1)S(1)}, bf16[24,512]{1,0:T(8,128)(2,1)S(1)}, u32[]{:S(2)}, u32[]{:S(2)}) collective-permute-start(bf16[24,512]{1,0:T(8,128)(2,1)S(1)} %get-tuple-element.60), channel_id=1, source_target_pairs={{1,0},{2,1},{3,2},{4,3},{5,4},{6,5},{7,6},{0,7},{9,8},{10,9},{11,1... | collective-permute-start | bytes 73736 | tf_op jit(solution)/shard_map/ppermute | solution.py:15
  165.5 1.7 collective-permute-start.7
  167.2 1.3 collective-permute-start.6
  168.6 2.1 %fusion.34 = f32[384,512]{1,0:T(8,128)S(1)} fusion(f32[512,512]{1,0:T(8,128)} %copy-done.14, f32[384,1024]{1,0:T(8,128)} %copy-done.12, bf16[1536,512]{1,0:T(8,128)(2,1)} %param.26, bf16[1,1,384,512]{3,2,1,0:T(8,128)(2,1)S(1)} %copy-done.13, bf16[896,512]{1,0:T(8,128)(2,1)} %copy-done.19), kind=kOutput, calls=%fused_computation.61 | convolution fusion | flops 202113024 | bytes 3670016 | tf_op jit(solution)/shard_map/dot_general | solution.py:120
  170.8 4.6 %collective-permute-done.4 = bf16[24,512]{1,0:T(8,128)(2,1)S(1)} collective-permute-done((bf16[24,512]{1,0:T(8,128)(2,1)S(1)}, bf16[24,512]{1,0:T(8,128)(2,1)S(1)}, u32[]{:S(2)}, u32[]{:S(2)}) %collective-permute-start.4) | collective-permute-done | bytes 24608 | tf_op jit(solution)/shard_map/ppermute | solution.py:15
  175.3 4.9 %collective-permute-done.5 = bf16[24,512]{1,0:T(8,128)(2,1)S(1)} collective-permute-done((bf16[24,512]{1,0:T(8,128)(2,1)S(1)}, bf16[24,512]{1,0:T(8,128)(2,1)S(1)}, u32[]{:S(2)}, u32[]{:S(2)}) %collective-permute-start.5) | collective-permute-done | bytes 24608 | tf_op jit(solution)/shard_map/ppermute | solution.py:15
  180.2 1.1 fusion.36
  182.9 8.0 %all-to-all-done.3 = bf16[32,64,512]{2,1,0:T(8,128)(2,1)S(1)} async-done(((bf16[32,64,512]{2,1,0:T(8,128)(2,1)}), bf16[32,64,512]{2,1,0:T(8,128)(2,1)S(1)}, u32[]{:S(2)}, u32[]{:S(2)}) %all-to-all-start.3) | async-done | bytes 2097184 | tf_op jit(solution)/shard_map/all_to_all | solution.py:105
  (146 shorter events, 16.9 us)
Async XLA Ops:
  0.6 47.1 %copy-start = (bf16[512,512]{1,0:T(8,128)(2,1)S(1)}, bf16[512,512]{1,0:T(8,128)(2,1)}, u32[]{:S(2)}) copy-start(bf16[512,512]{1,0:T(8,128)(2,1)} %param.28) | copy-start | bytes 1572868
  0.7 25.2 %copy-start.3 = (bf16[1,1,384,512]{3,2,1,0:T(8,128)(2,1)S(1)}, bf16[1,1,384,512]{3,2,1,0:T(8,128)(2,1)}, u32[]{:S(2)}) copy-start(bf16[1,1,384,512]{3,2,1,0:T(8,128)(2,1)} %param.17) | copy-start | bytes 1179652
  0.7 25.2 %copy-start.11 = (bf16[1024,512]{1,0:T(8,128)(2,1)S(1)}, bf16[1024,512]{1,0:T(8,128)(2,1)}, u32[]{:S(2)}) copy-start(bf16[1024,512]{1,0:T(8,128)(2,1)} %param.30) | copy-start | bytes 3145732
  0.7 25.2 %copy-start.35 = (f32[512]{0:T(512)S(1)}, f32[512]{0:T(512)}, u32[]{:S(2)}) copy-start(f32[512]{0:T(512)} %param.31) | copy-start | bytes 6148
  2.2 34.1 %all-to-all-start = ((bf16[32,2,512]{2,1,0:T(2,128)(2,1)}), bf16[32,2,512]{2,1,0:T(2,128)(2,1)S(1)}, u32[]{:S(2)}, u32[]{:S(2)}) async-start(bf16[32,2,512]{2,1,0:T(2,128)(2,1)} %broadcast_in_dim.47), calls=%async_computation | async-start | bytes 131072 | tf_op jit(solution)/shard_map/all_to_all | solution.py:105
  10.3 13.3 %copy-start.31 = (s32[96]{0:T(128)}, s32[96]{0:T(128)S(1)}, u32[]{:S(2)}) copy-start(s32[96]{0:T(128)S(1)} %eq.147) | copy-start | bytes 1156
  11.6 24.7 %collective-permute-start.3 = (bf16[24,512]{1,0:T(8,128)(2,1)S(1)}, bf16[24,512]{1,0:T(8,128)(2,1)S(1)}, u32[]{:S(2)}, u32[]{:S(2)}) collective-permute-start(bf16[24,512]{1,0:T(8,128)(2,1)S(1)} %get-tuple-element.66), channel_id=1, source_target_pairs={{8,0},{16,8},{24,16},{9,1},{17,9},{25,17},{10,2},{18,10},{26,18},{... | collective-permute-start | bytes 73736 | tf_op jit(solution)/shard_map/ppermute | solution.py:21
  12.9 23.4 %collective-permute-start.2 = (bf16[24,512]{1,0:T(8,128)(2,1)S(1)}, bf16[24,512]{1,0:T(8,128)(2,1)S(1)}, u32[]{:S(2)}, u32[]{:S(2)}) collective-permute-start(bf16[24,512]{1,0:T(8,128)(2,1)S(1)} %get-tuple-element.67), channel_id=1, source_target_pairs={{0,8},{8,16},{16,24},{1,9},{9,17},{17,25},{2,10},{10,18},{18,26},{... | collective-permute-start | bytes 73736 | tf_op jit(solution)/shard_map/ppermute | solution.py:21
  15.9 20.4 %collective-permute-start.1 = (bf16[24,512]{1,0:T(8,128)(2,1)S(1)}, bf16[24,512]{1,0:T(8,128)(2,1)S(1)}, u32[]{:S(2)}, u32[]{:S(2)}) collective-permute-start(bf16[24,512]{1,0:T(8,128)(2,1)S(1)} %get-tuple-element.68), channel_id=1, source_target_pairs={{1,0},{2,1},{3,2},{4,3},{5,4},{6,5},{7,6},{0,7},{9,8},{10,9},{11,1... | collective-permute-start | bytes 73736 | tf_op jit(solution)/shard_map/ppermute | solution.py:15
  20.5 15.0 %collective-permute-start = (bf16[24,512]{1,0:T(8,128)(2,1)S(1)}, bf16[24,512]{1,0:T(8,128)(2,1)}, u32[]{:S(2)}, u32[]{:S(2)}) collective-permute-start(bf16[24,512]{1,0:T(8,128)(2,1)S(1)} %get-tuple-element.69), channel_id=1, source_target_pairs={{7,0},{0,1},{1,2},{2,3},{3,4},{4,5},{5,6},{6,7},{15,8},{8,9},{9,10... | collective-permute-start | bytes 73736 | tf_op jit(solution)/shard_map/ppermute | solution.py:15
  22.9 13.6 %copy-start.36 = (pred[32]{0:T(512)(128)(4,1)}, pred[32]{0:T(512)(128)(4,1)S(1)}, u32[]{:S(2)}) copy-start(pred[32]{0:T(512)(128)(4,1)S(1)} %get-tuple-element.76) | copy-start | bytes 100
  22.9 13.6 %copy-start.38 = (pred[32]{0:T(512)(128)(4,1)}, pred[32]{0:T(512)(128)(4,1)S(1)}, u32[]{:S(2)}) copy-start(pred[32]{0:T(512)(128)(4,1)S(1)} %get-tuple-element.77) | copy-start | bytes 100
  26.2 27.1 %copy-start.33 = (pred[3072]{0:T(1024)(128)(4,1)}, pred[3072]{0:T(1024)(128)(4,1)S(1)}, u32[]{:S(2)}) copy-start(pred[3072]{0:T(1024)(128)(4,1)S(1)} %get-tuple-element.91) | copy-start | bytes 9220
  36.5 7.2 %copy-start.26 = (bf16[512,512]{1,0:T(8,128)(2,1)}, bf16[512,512]{1,0:T(8,128)(2,1)S(1)}, u32[]{:S(2)}) copy-start(bf16[512,512]{1,0:T(8,128)(2,1)S(1)} %fusion.93) | copy-start | bytes 1572868
  38.2 5.5 %copy-start.17 = (bf16[1,1,3072,512]{3,2,1,0:T(8,128)(2,1)S(1)}, bf16[1,1,3072,512]{3,2,1,0:T(8,128)(2,1)}, u32[]{:S(2)}) copy-start(bf16[1,1,3072,512]{3,2,1,0:T(8,128)(2,1)} %param.18) | copy-start | bytes 9437188
  38.2 5.5 %copy-start.20 = (bf16[1536,512]{1,0:T(8,128)(2,1)S(1)}, bf16[1536,512]{1,0:T(8,128)(2,1)}, u32[]{:S(2)}) copy-start(bf16[1536,512]{1,0:T(8,128)(2,1)} %param.26) | copy-start | bytes 4718596
  38.3 5.5 %copy-start.42 = (f32[512]{0:T(512)S(1)}, f32[512]{0:T(512)}, u32[]{:S(2)}) copy-start(f32[512]{0:T(512)} %param.27) | copy-start | bytes 6148
  47.8 2.0 %copy-start.7 = (bf16[3072,512]{1,0:T(8,128)(2,1)}, bf16[3072,512]{1,0:T(8,128)(2,1)S(1)}, u32[]{:S(2)}) copy-start(bf16[3072,512]{1,0:T(8,128)(2,1)S(1)} %get-tuple-element.78) | copy-start | bytes 9437188
  49.7 1.9 copy-start.5
  49.8 1.9 copy-start.29
  53.4 2.1 %copy-start.40 = (bf16[512,512]{1,0:T(8,128)(2,1)S(1)}, bf16[512,512]{1,0:T(8,128)(2,1)}, u32[]{:S(2)}) copy-start(bf16[512,512]{1,0:T(8,128)(2,1)} %param.32) | copy-start | bytes 1572868
  55.5 2.9 %copy-start.22 = (f32[384,512]{1,0:T(8,128)}, f32[384,512]{1,0:T(8,128)S(1)}, u32[]{:S(2)}) copy-start(f32[384,512]{1,0:T(8,128)S(1)} %convolution_add_fusion.1) | copy-start | bytes 2359300
  58.4 2.0 %copy-start.18 = (bf16[1,1,3072,512]{2,3,1,0:T(8,128)(2,1)S(1)}, bf16[1,1,3072,512]{2,3,1,0:T(8,128)(2,1)}, u32[]{:S(2)}) copy-start(bf16[1,1,3072,512]{2,3,1,0:T(8,128)(2,1)} %copy.42) | copy-start | bytes 9437188
  58.4 2.0 %copy-start.34 = (pred[3072]{0:T(1024)(128)(4,1)S(1)}, pred[3072]{0:T(1024)(128)(4,1)}, u32[]{:S(2)}) copy-start(pred[3072]{0:T(1024)(128)(4,1)} %copy-done.33) | copy-start | bytes 9220
  59.0 8.5 %slice-start = ((s8[6291456]{0:T(1024)(128)(4,1)}), s8[4194304]{0:T(1024)(128)(4,1)S(1)}, s32[]{:S(2)}) async-start(s8[6291456]{0:T(1024)(128)(4,1)} %bitcast.114), calls=%async_computation.4 | async-start | bytes 8388608
  60.4 4.4 %copy-start.12 = (f32[384,1024]{1,0:T(8,128)}, f32[384,1024]{1,0:T(8,128)S(1)}, u32[]{:S(2)}) copy-start(f32[384,1024]{1,0:T(8,128)S(1)} %fusion.105) | copy-start | bytes 4718596
  60.4 7.0 %slice-start.1 = ((s8[6291456]{0:T(1024)(128)(4,1)}), s8[2097152]{0:T(1024)(128)(4,1)S(1)}, s32[]{:S(2)}) async-start(s8[6291456]{0:T(1024)(128)(4,1)} %bitcast.114), calls=%async_computation.5 | async-start | bytes 4194304
  64.8 2.6 %copy-start.2 = (f32[3072,512]{0,1:T(8,128)}, f32[3072,512]{0,1:T(8,128)S(1)}, u32[]{:S(2)}) copy-start(f32[3072,512]{0,1:T(8,128)S(1)} %get-tuple-element.84) | copy-start | bytes 18874372
  67.4 4.4 %copy-start.15 = (bf16[3072,512]{0,1:T(8,128)(2,1)}, bf16[3072,512]{0,1:T(8,128)(2,1)S(1)}, u32[]{:S(2)}) copy-start(bf16[3072,512]{0,1:T(8,128)(2,1)S(1)} %multiply_convert_fusion.1) | copy-start | bytes 9437188
  71.8 1.8 copy-start.6
  73.6 3.0 %copy-start.27 = (bf16[512,512]{1,0:T(8,128)(2,1)S(1)}, bf16[512,512]{1,0:T(8,128)(2,1)}, u32[]{:S(2)}) copy-start(bf16[512,512]{1,0:T(8,128)(2,1)} %copy-done.26) | copy-start | bytes 1572868
  76.7 3.4 %copy-start.37 = (pred[32]{0:T(512)(128)(4,1)S(1)}, pred[32]{0:T(512)(128)(4,1)}, u32[]{:S(2)}) copy-start(pred[32]{0:T(512)(128)(4,1)} %copy-done.36) | copy-start | bytes 100
  76.7 3.4 %copy-start.39 = (pred[32]{0:T(512)(128)(4,1)S(1)}, pred[32]{0:T(512)(128)(4,1)}, u32[]{:S(2)}) copy-start(pred[32]{0:T(512)(128)(4,1)} %copy-done.38) | copy-start | bytes 100
  79.8 15.2 %copy-start.14 = (f32[512,512]{1,0:T(8,128)}, f32[512,512]{1,0:T(8,128)S(1)}, u32[]{:S(2)}) copy-start(f32[512,512]{1,0:T(8,128)S(1)} %get-tuple-element.90) | copy-start | bytes 3145732
  81.2 13.8 %all-to-all-start.1 = ((bf16[32,3,512]{2,1,0:T(4,128)(2,1)}), bf16[32,3,512]{2,1,0:T(4,128)(2,1)S(1)}, u32[]{:S(2)}, u32[]{:S(2)}) async-start(bf16[32,3,512]{2,1,0:T(4,128)(2,1)} %copy.43), calls=%async_computation.1 | async-start | bytes 262144 | tf_op jit(solution)/shard_map/all_to_all | solution.py:105
  95.0 41.5 %all-to-all-start.2 = ((bf16[32,48,512]{2,1,0:T(8,128)(2,1)}), bf16[32,48,512]{2,1,0:T(8,128)(2,1)S(1)}, u32[]{:S(2)}, u32[]{:S(2)}) async-start(bf16[32,48,512]{2,1,0:T(8,128)(2,1)} %bitcast.105), calls=%async_computation.2 | async-start | bytes 3145728 | tf_op jit(solution)/shard_map/all_to_all | solution.py:105
  97.9 2.2 %copy-start.23 = (f32[384,512]{1,0:T(8,128)S(1)}, f32[384,512]{1,0:T(8,128)}, u32[]{:S(2)}) copy-start(f32[384,512]{1,0:T(8,128)} %copy-done.22) | copy-start | bytes 2359300
  97.9 2.2 %copy-start.25 = (bf16[384,512]{1,0:T(8,128)(2,1)S(1)}, bf16[384,512]{1,0:T(8,128)(2,1)}, u32[]{:S(2)}) copy-start(bf16[384,512]{1,0:T(8,128)(2,1)} %copy-done.24) | copy-start | bytes 1179652
  100.0 1.9 copy-start.8
  100.0 2.8 %copy-start.16 = (bf16[3072,512]{0,1:T(8,128)(2,1)S(1)}, bf16[3072,512]{0,1:T(8,128)(2,1)}, u32[]{:S(2)}) copy-start(bf16[3072,512]{0,1:T(8,128)(2,1)} %copy-done.15) | copy-start | bytes 9437188
  137.6 53.3 %all-to-all-start.3 = ((bf16[32,64,512]{2,1,0:T(8,128)(2,1)}), bf16[32,64,512]{2,1,0:T(8,128)(2,1)S(1)}, u32[]{:S(2)}, u32[]{:S(2)}) async-start(bf16[32,64,512]{2,1,0:T(8,128)(2,1)} %pad_maximum_fusion), calls=%async_computation.3 | async-start | bytes 4194304 | tf_op jit(solution)/shard_map/all_to_all | solution.py:105
  160.0 20.3 %copy-start.32 = (s32[96]{0:T(128)S(1)}, s32[96]{0:T(128)}, u32[]{:S(2)}) copy-start(s32[96]{0:T(128)} %copy-done.31) | copy-start | bytes 1156
  160.0 22.1 %copy-start.10 = (bf16[32,48,512]{2,1,0:T(8,128)(2,1)S(1)}, bf16[32,48,512]{2,1,0:T(8,128)(2,1)}, u32[]{:S(2)}) copy-start(bf16[32,48,512]{2,1,0:T(8,128)(2,1)} %copy-done.9) | copy-start | bytes 4718596
  160.9 14.5 %collective-permute-start.4 = (bf16[24,512]{1,0:T(8,128)(2,1)S(1)}, bf16[24,512]{1,0:T(8,128)(2,1)S(1)}, u32[]{:S(2)}, u32[]{:S(2)}) collective-permute-start(bf16[24,512]{1,0:T(8,128)(2,1)S(1)} %get-tuple-element.60), channel_id=1, source_target_pairs={{1,0},{2,1},{3,2},{4,3},{5,4},{6,5},{7,6},{0,7},{9,8},{10,9},{11,1... | collective-permute-start | bytes 73736 | tf_op jit(solution)/shard_map/ppermute | solution.py:15
  165.5 9.9 %collective-permute-start.7 = (bf16[24,512]{1,0:T(8,128)(2,1)S(1)}, bf16[24,512]{1,0:T(8,128)(2,1)S(1)}, u32[]{:S(2)}, u32[]{:S(2)}) collective-permute-start(bf16[24,512]{1,0:T(8,128)(2,1)S(1)} %get-tuple-element.61), channel_id=1, source_target_pairs={{0,8},{8,16},{16,24},{1,9},{9,17},{17,25},{2,10},{10,18},{18,26},{... | collective-permute-start | bytes 73736 | tf_op jit(solution)/shard_map/ppermute | solution.py:21
  167.2 8.1 %collective-permute-start.6 = (bf16[24,512]{1,0:T(8,128)(2,1)S(1)}, bf16[24,512]{1,0:T(8,128)(2,1)S(1)}, u32[]{:S(2)}, u32[]{:S(2)}) collective-permute-start(bf16[24,512]{1,0:T(8,128)(2,1)S(1)} %get-tuple-element.62), channel_id=1, source_target_pairs={{8,0},{16,8},{24,16},{9,1},{17,9},{25,17},{10,2},{18,10},{26,18},{... | collective-permute-start | bytes 73736 | tf_op jit(solution)/shard_map/ppermute | solution.py:21
  168.5 11.7 %collective-permute-start.5 = (bf16[24,512]{1,0:T(8,128)(2,1)S(1)}, bf16[24,512]{1,0:T(8,128)(2,1)S(1)}, u32[]{:S(2)}, u32[]{:S(2)}) collective-permute-start(bf16[24,512]{1,0:T(8,128)(2,1)S(1)} %get-tuple-element.63), channel_id=1, source_target_pairs={{7,0},{0,1},{1,2},{2,3},{3,4},{4,5},{5,6},{6,7},{15,8},{8,9},{9,10... | collective-permute-start | bytes 73736 | tf_op jit(solution)/shard_map/ppermute | solution.py:15
  168.6 23.9 %copy-start.1 = (bf16[512,512]{1,0:T(8,128)(2,1)S(1)}, bf16[512,512]{1,0:T(8,128)(2,1)}, u32[]{:S(2)}) copy-start(bf16[512,512]{1,0:T(8,128)(2,1)} %param.28) | copy-start | bytes 1572868
  (9 other events, 13.0 us)
where the time goes:
time: 194 us; the launch traced here: 193 us
  waiting for transfers between devices  53.2 us (27%)
  matrix products  52.9 us (27%)
  starting transfers between devices  35.6 us (18%)
  local copies, waits for them, and re-layouts  35.3 us (18%)
  other arithmetic  13.4 us (7%)
  between operations  2.09 us (1%)
    all_to_all x4, waiting for transfers between devices, exchange(): return lax.all_to_all(value, axes, split_axis=0, concat_axis=0, tiled=True)  43.8 us
    dot_general x14, matrix products, product(): return jnp.dot(left, right, preferred_element_type=jnp.float32)  42.6 us
    unnamed x99, local copies, waits for them, and re-layouts  29.1 us
    all_to_all x4, starting transfers between devices, exchange(): return lax.all_to_all(value, axes, split_axis=0, concat_axis=0, tiled=True)  19 us
    ppermute x4, waiting for transfers between devices, shifted(): return lax.ppermute(block, axis, route)  9.44 us
    ppermute x4, starting transfers between devices, shifted(): return lax.ppermute(block, axis, route)  9.26 us
    dot_general x7, matrix products, transposed(): lax.dot_general(left, right, (((0,), (0,)), ((), ())), preferred_element_...  7.99 us
    ppermute x4, starting transfers between devices, passed_along(): lax.ppermute(value, axis, [(source, source + steps) for source in range(l...  7.35 us
  transfers between devices with their start and end apart: 12, of which 5 were waited for; matrix products, arithmetic and copies ran while one was open for 26% of the time, Pallas kernels for 0%

commit v1 on v0

v1 whole, which is shorter than its diff:
```python
import functools

import jax
import jax.numpy as jnp
from jax import lax
from jax.experimental import pallas as pl
from jax.experimental.pallas import tpu as pltpu
from jax.sharding import PartitionSpec as P

COARSE = 2
EPS = 1e-05
LANES = 128
TILE = 512
BF = jnp.bfloat16
F32 = jnp.float32
VMEM = pltpu.VMEM


def dot(a, b):
    return jnp.dot(a, b, preferred_element_type=F32)


def dot_nt(a, b):
    return lax.dot_general(a, b, (((1,), (1,)), ((), ())), preferred_element_type=F32)


def dot_tn(a, b):
    return lax.dot_general(a, b, (((0,), (0,)), ((), ())), preferred_element_type=F32)


def iota(shape, dim):
    return lax.broadcasted_iota(jnp.int32, shape, dim)


def onehot(mask):
    return jnp.where(mask, 1.0, 0.0).astype(BF)


def up(n, m):
    return -(-n // m) * m


class Sizes:
    def __init__(self, mesh, node_n, halo_n, slot_n):
        self.lat, self.lon = mesh.shape["lat"], mesh.shape["lon"]
        self.dev = self.lat * self.lon
        self.node = node_n
        self.halo = halo_n
        self.hslot = up(halo_n, 16)
        self.hrows = up(4 * self.hslot, LANES)
        self.slot = slot_n
        self.far_n = self.dev * slot_n
        self.far = up(self.far_n, LANES)
        self.recv_at = node_n + self.hrows
        self.far_at = self.recv_at + node_n
        self.cols = self.far_at + self.far
        self.core = 2 if self.lat % 2 == 0 else 1
        self.x = self.lat // self.core
        self.y = 2 if self.lon % 2 == 0 else 1
        self.z = self.lon // self.y


def flat_device(s, r):
    return {"lat": r // s.lon, "lon": r % s.lon}


def remote(src, dst, send, recv, peer):
    return pltpu.make_async_remote_copy(
        src_ref=src,
        dst_ref=dst,
        send_sem=send,
        recv_sem=recv,
        device_id=peer,
        device_id_type=pl.DeviceIdType.MESH,
    )


def neighbours(s):
    a, b = lax.axis_index("lat"), lax.axis_index("lon")
    east, west = (b + 1) % s.lon, (b + s.lon - 1) % s.lon
    south, north = (a + 1) % s.lat, (a + s.lat - 1) % s.lat
    return [
        {"lat": a, "lon": east},
        {"lat": a, "lon": west},
        {"lat": south, "lon": b},
        {"lat": north, "lon": b},
    ]


def coarse_rows(s, need, q, width):
    spot = (iota((1, s.far), 1) // s.slot) * (COARSE * width // LANES)
    row = jnp.where(need < 0, -1, spot + need * (width // LANES) + q)
    return onehot(iota((s.dev * COARSE * width // LANES, s.far), 0) == row)


def table_kernel(
    s, nodes, out_rows, need, ext, own, sent, came, far_in, send_h, recv_h, send_c, recv_c
):
    width = nodes.shape[1]
    cuts = width // LANES
    a, b = lax.axis_index("lat"), lax.axis_index("lon")
    me = a * s.lon + b
    barrier = pltpu.get_barrier_semaphore()

    def greet(d, _):
        pl.semaphore_signal(
            barrier, 1, device_id=flat_device(s, (me + d) % s.dev), device_id_type=pl.DeviceIdType.MESH
        )
        return 0

    lax.fori_loop(1, s.dev, greet, 0)
    top = nodes[0:16, :].astype(F32)
    for c in range(COARSE):
        for q in range(cuts):
            j = c * cuts + q
            own[j : j + 1, :] = top[c : c + 1, q * LANES : (q + 1) * LANES]
    pick = onehot(iota((s.node, s.hrows), 0) == out_rows[0:1, :])
    sent[...] = dot_tn(pick, nodes[...]).astype(BF)
    pl.semaphore_wait(barrier, s.dev - 1)
    copies = []
    for k, peer in enumerate(neighbours(s)):
        rows = pl.ds(k * s.hslot, s.hslot)
        copies.append(remote(sent.at[rows], came.at[rows], send_h.at[k], recv_h.at[k], peer))
        copies[-1].start()
    units = COARSE * cuts

    def coarse_copy(d):
        return remote(
            own,
            far_in.at[pl.ds(me * units, units)],
            send_c.at[d],
            recv_c.at[d],
            flat_device(s, (me + d) % s.dev),
        )

    def push(d, _):
        coarse_copy(d).start()
        return 0

    lax.fori_loop(1, s.dev, push, 0)
    far_in[pl.ds(me * units, units), :] = own[...]
    for copy in copies:
        copy.wait()
    block = iota((s.hrows, 1), 0) // s.hslot
    dead = ((block == 2) & (a == 0)) | ((block == 3) & (a == s.lat - 1))
    ext[0 : s.hrows, :] = jnp.where(dead, 0.0, came[...].astype(F32)).astype(BF)

    def settle(d, _):
        coarse_copy(d).wait()
        return 0

    lax.fori_loop(1, s.dev, settle, 0)
    rows = far_in[...].astype(BF)
    for q in range(cuts):
        pick = coarse_rows(s, need[0:1, :], q, width)
        ext[s.hrows :, q * LANES : (q + 1) * LANES] = dot_tn(pick, rows).astype(BF)


def exchange_table(s, nodes, out_rows, need):
    width = nodes.shape[1]
    units = COARSE * width // LANES
    full = pl.BlockSpec(memory_space=VMEM)
    return pl.pallas_call(
        functools.partial(table_kernel, s),
        out_shape=jax.ShapeDtypeStruct((s.hrows + s.far, width), BF),
        in_specs=[full] * 3,
        out_specs=full,
        scratch_shapes=[
            VMEM((units, LANES), F32),
            VMEM((s.hrows, width), BF),
            VMEM((s.hrows, width), BF),
            VMEM((s.dev * units, LANES), F32),
            pltpu.SemaphoreType.DMA((4,)),
            pltpu.SemaphoreType.DMA((4,)),
            pltpu.SemaphoreType.DMA((s.dev,)),
            pltpu.SemaphoreType.DMA((s.dev,)),
        ],
        compiler_params=pltpu.CompilerParams(collective_id=0, has_side_effects=True),
        name="table",
    )(nodes, out_rows, need)


def normalise(z):
    mean = jnp.mean(z, axis=-1, keepdims=True)
    centred = z - mean
    rstd = lax.rsqrt(jnp.mean(centred * centred, axis=-1, keepdims=True) + EPS)
    return centred * rstd, rstd


def gate(z):
    sig = 1.0 / (1.0 + jnp.exp(-z))
    return (z * sig).astype(BF), sig * (1.0 + z * (1.0 - sig))


def norm_back(scaled, normed, rstd):
    return rstd * (
        scaled
        - jnp.mean(scaled, axis=-1, keepdims=True)
        - normed * jnp.mean(scaled * normed, axis=-1, keepdims=True)
    )


def layer_kernel(
    s,
    count,
    snd,
    rcv,
    nodes,
    ext,
    edges,
    edge_cot,
    node_cot,
    e_w1,
    e_b1,
    e_w2,
    e_gain,
    n_w1,
    n_b1,
    n_w2,
    n_gain,
    new_edges,
    edge_grad,
    new_nodes,
    node_part,
    ext_grad,
    early,
    late,
    vectors,
    snd_s,
    rcv_s,
    mix,
    pick,
    pick_t,
    active,
    slope,
    normed,
    rstd,
    agg,
    g_agg,
    spread,
    w_edge_grad,
    w_two_grad,
):
    i = pl.program_id(0)
    width = nodes.shape[1]
    steps = pick.shape[0]
    tile = pick.shape[1]
    groups = tile // LANES
    dev = s.dev

    @pl.when(i == 0)
    def _():
        lives = snd_s.shape[0] * LANES
        place = iota(snd_s.shape, 0) * LANES + iota(snd_s.shape, 1)
        live = place < count[0, 0]
        ids = snd[...]
        base = s.node
        moved = ids
        for k in range(1, 4):
            moved = moved + jnp.where(ids >= base + k * s.halo, s.hslot - s.halo, 0)
        ends = base + 4 * s.halo
        moved = jnp.where(ids >= ends, ids - ends + s.far_at, moved)
        snd_s[...] = jnp.where(live, moved, -1)
        rcv_s[...] = jnp.where(live, rcv[...] + s.recv_at, -1)
        mix[0:width, :] = e_w1[0:width, :]
        w_send, w_recv = e_w1[width : 2 * width, :], e_w1[2 * width :, :]
        at = width
        mix[at : at + s.node, :] = dot(nodes[...], w_send).astype(BF)
        mix[at + s.node : at + s.recv_at, :] = dot(ext[0 : s.hrows, :], w_send).astype(BF)
        mix[at + s.recv_at : at + s.far_at, :] = dot(nodes[...], w_recv).astype(BF)
        mix[at + s.far_at :, :] = dot(ext[s.hrows :, :], w_send).astype(BF)
        agg[...] = jnp.zeros_like(agg)
        spread[...] = jnp.zeros_like(spread)
        w_edge_grad[...] = jnp.zeros_like(w_edge_grad)
        w_two_grad[...] = jnp.zeros_like(w_two_grad)
        vectors[...] = jnp.zeros_like(vectors)

    def rows_of(c):
        return s.recv_at <= c < s.far_at

    @pl.when(i < steps)
    def _():
        live = (iota((tile, 1), 0) + i * tile) < count[0, 0]
        for g in range(groups):
            at = i * groups + g
            srow, rrow = snd_s[pl.ds(at, 1), :], rcv_s[pl.ds(at, 1), :]
            scol = jnp.broadcast_to(srow, (LANES, LANES)).T
            rcol = jnp.broadcast_to(rrow, (LANES, LANES)).T
            lane = iota((LANES, LANES), 1)
            sub = iota((LANES, LANES), 0)
            span = slice(g * LANES, (g + 1) * LANES)
            for c in range(0, s.cols, LANES):
                col, row = (rcol, rrow) if rows_of(c) else (scol, srow)
                pick[i, span, c : c + LANES] = onehot(lane + c == col)
                pick_t[i, c : c + LANES, span] = onehot(sub + c == row)
        e = edges[...]
        z = dot(jnp.concatenate([e, pick[i]], axis=1), mix[...]) + e_b1[...]
        act, back = gate(z)
        active[i] = act
        slope[i] = back.astype(BF)
        unit, scale = normalise(dot(act, e_w2[...]))
        normed[i] = unit.astype(BF)
        rstd[i] = scale
        fresh = (e.astype(F32) + jnp.where(live, unit * e_gain[...], 0.0)).astype(BF)
        new_edges[...] = fresh
        agg[...] += dot(pick_t[i, s.recv_at : s.far_at, :], fresh)

    @pl.when(i == steps - 1)
    def _():
        own = nodes[...]
        both = jnp.concatenate([own, agg[...].astype(BF)], axis=1)
        act, back = gate(dot(both, n_w1[...]) + n_b1[...])
        unit, scale = normalise(dot(act, n_w2[...]))
        new_nodes[...] = (own.astype(F32) + unit * n_gain[...]).astype(BF)
        g = node_cot[...].astype(F32)
        vectors[3:4, :] = jnp.sum(g * unit, axis=0, keepdims=True)
        g_two = norm_back(g * n_gain[...], unit, scale).astype(BF)
        n_two = dot_tn(act, g_two).astype(BF)
        g_one = (dot_nt(g_two, n_w2[...]) * back).astype(BF)
        vectors[2:3, :] = jnp.sum(g_one.astype(F32), axis=0, keepdims=True)
        n_one = dot_tn(both, g_one).astype(BF)
        g_in = dot_nt(g_one, n_w1[...])
        node_part[...] = g + g_in[:, :width]
        g_agg[...] = g_in[:, width:].astype(BF)
        one, two = n_one.shape[0] // dev, n_two.shape[0] // dev
        for d in range(dev):
            early[d, 0:one, :] = n_one[d * one : (d + 1) * one, :]
            early[d, one : one + two, :] = n_two[d * two : (d + 1) * two, :]

    @pl.when(i >= steps)
    def _():
        t = i - steps
        live = (iota((tile, 1), 0) + t * tile) < count[0, 0]
        d_new = edge_cot[...].astype(F32) + dot(pick[t, :, s.recv_at : s.far_at], g_agg[...])
        g = jnp.where(live, d_new, 0.0)
        unit = normed[t].astype(F32)
        vectors[1:2, :] += jnp.sum(g * unit, axis=0, keepdims=True)
        g_two = norm_back(g * e_gain[...], unit, rstd[t]).astype(BF)
        w_two_grad[...] += dot_tn(active[t], g_two)
        g_one = (dot_nt(g_two, e_w2[...]) * slope[t].astype(F32)).astype(BF)
        vectors[0:1, :] += jnp.sum(g_one.astype(F32), axis=0, keepdims=True)
        w_edge_grad[...] += dot_tn(edges[...], g_one)
        spread[...] += dot(pick_t[t], g_one)
        edge_grad[...] = d_new + dot_nt(g_one, e_w1[0:width, :])

    @pl.when(i == 2 * steps - 1)
    def _():
        w_send, w_recv = e_w1[width : 2 * width, :], e_w1[2 * width :, :]
        own = nodes[...]
        s_own = spread[0 : s.node, :].astype(BF)
        s_halo = spread[s.node : s.recv_at, :].astype(BF)
        s_recv = spread[s.recv_at : s.far_at, :].astype(BF)
        s_far = spread[s.far_at :, :].astype(BF)
        late[0:width, :] = w_edge_grad[...].astype(BF)
        late[width : 2 * width, :] = (
            dot_tn(own, s_own) + dot_tn(ext[0 : s.hrows, :], s_halo) + dot_tn(ext[s.hrows :, :], s_far)
        ).astype(BF)
        late[2 * width :, :] = dot_tn(own, s_recv).astype(BF)
        two = w_two_grad.shape[0] // dev
        at = early.shape[1] - two
        for d in range(dev):
            early[d, at:, :] = w_two_grad[d * two : (d + 1) * two, :].astype(BF)
        node_part[...] += dot_nt(s_own, w_send) + dot_nt(s_recv, w_recv)
        ext_grad[0 : s.hrows, :] = dot_nt(s_halo, w_send).astype(BF)
        ext_grad[s.hrows :, :] = dot_nt(s_far, w_send).astype(BF)


def layer(s, count, snd, rcv, nodes, ext, edges, edge_cot, node_cot, weights):
    edge_n, width = edges.shape
    hidden = weights[2].shape[0]
    steps = edge_n // TILE
    whole = pl.BlockSpec(memory_space=VMEM)
    smem = pl.BlockSpec(memory_space=pltpu.SMEM)
    once = functools.partial(pl.BlockSpec, pipeline_mode=pl.Buffered(1))

    def fixed(shape):
        return once(shape, lambda i: (0,) * len(shape))

    def tile(index):
        return pl.BlockSpec((TILE, width), lambda i: (index(i), 0))

    both = tile(lambda i: lax.rem(i, steps))
    first = tile(lambda i: jnp.minimum(i, steps - 1))
    second = tile(lambda i: jnp.maximum(i - steps, 0))
    inputs = (count, snd, rcv, nodes, ext, edges, edge_cot, node_cot) + weights
    in_specs = [smem] + [fixed(v.shape) for v in inputs[1:]]
    in_specs[5], in_specs[6] = both, second
    per = (weights[4].shape[0] + weights[6].shape[0] + weights[2].shape[0]) // s.dev
    late_n = weights[0].shape[0]
    out = [
        ((edge_n, width), BF, first),
        ((edge_n, width), F32, second),
        (nodes.shape, BF, None),
        (nodes.shape, F32, None),
        ((s.hrows + s.far, width), BF, None),
        ((s.dev, per, width), BF, None),
        ((late_n, width), BF, None),
        ((8, width), F32, None),
    ]
    return pl.pallas_call(
        functools.partial(layer_kernel, s),
        grid=(2 * steps,),
        out_shape=[jax.ShapeDtypeStruct(shape, kind) for shape, kind, _ in out],
        in_specs=in_specs,
        out_specs=[spec or fixed(shape) for shape, _, spec in out],
        scratch_shapes=[
            VMEM(snd.shape, jnp.int32),
            VMEM(snd.shape, jnp.int32),
            VMEM((width + s.cols, hidden), BF),
            VMEM((steps, TILE, s.cols), BF),
            VMEM((steps, s.cols, TILE), BF),
            VMEM((steps, TILE, hidden), BF),
            VMEM((steps, TILE, hidden), BF),
            VMEM((steps, TILE, width), BF),
            VMEM((steps, TILE, 1), F32),
            VMEM((s.node, width), F32),
            VMEM((s.node, width), BF),
            VMEM((s.cols, hidden), F32),
            VMEM((width, hidden), F32),
            VMEM((hidden, width), F32),
        ],
        compiler_params=pltpu.CompilerParams(
            dimension_semantics=("arbitrary",), vmem_limit_bytes=63 * 1024 * 1000
        ),
        name="layer",
    )(*inputs)


def reduce_kernel(
    s,
    out_rows,
    need,
    node_part,
    ext_grad,
    early,
    late,
    vectors,
    node_grad,
    early_out,
    late_out,
    vec_out,
    fold,
    back,
    e0,
    l0,
    f0,
    v0,
    e1,
    l1,
    f1,
    v1,
    er1,
    lr1,
    fr1,
    vr1,
    e2,
    l2,
    f2,
    v2,
    er2,
    lr2,
    fr2,
    vr2,
    send_h,
    recv_h,
    send0,
    recv0,
    send1,
    recv1,
    send2,
    recv2,
):
    width = node_part.shape[1]
    cuts = width // LANES
    units = COARSE * cuts
    a, b = lax.axis_index("lat"), lax.axis_index("lon")
    x, core = a // s.core, a % s.core
    z, y = b // s.y, b % s.y
    barrier = pltpu.get_barrier_semaphore()
    around = neighbours(s)
    partner = {"lat": x * s.core + (core + 1) % s.core, "lon": b}
    plane = [(dx, dy) for dx in range(s.x) for dy in range(s.y) if dx or dy]

    def plane_peer(dx, dy):
        return {
            "lat": ((x + dx) % s.x) * s.core + core,
            "lon": z * s.y + (y + dy) % s.y,
        }

    def line_peer(dz):
        return {"lat": a, "lon": ((z + dz) % s.z) * s.y + y}

    peers = around + [partner] + [plane_peer(*p) for p in plane]
    peers = peers + [line_peer(dz) for dz in range(1, s.z)]
    for peer in peers:
        pl.semaphore_signal(barrier, 1, device_id=peer, device_id_type=pl.DeviceIdType.MESH)
    far = ext_grad[s.hrows :, :]
    total = jnp.zeros(fold.shape, F32)
    for q in range(cuts):
        total = total + dot(
            coarse_rows(s, need[0:1, :], q, width), far[:, q * LANES : (q + 1) * LANES]
        )
    fold[...] = total
    pl.semaphore_wait(barrier, len(peers))
    copies = []
    homes = [around[1], around[0], around[3], around[2]]
    for k, peer in enumerate(homes):
        rows = pl.ds(k * s.hslot, s.hslot)
        copies.append(remote(ext_grad.at[rows], back.at[rows], send_h.at[k], recv_h.at[k], peer))
    block = s.z * s.y
    other = (core + 1) % s.core
    stage0 = []
    for xx in range(s.x):
        rows = pl.ds((xx * s.core + other) * block, block)
        stage0.append(remote(early.at[rows], e0.at[xx], send0.at[0, xx], recv0.at[0, xx], partner))
        per = late.shape[0] // s.dev
        stage0.append(remote(late.at[rows], l0.at[xx], send0.at[1, xx], recv0.at[1, xx], partner))
        stage0.append(
            remote(
                fold.at[pl.ds((xx * s.core + other) * block * units, block * units)],
                f0.at[xx],
                send0.at[2, xx],
                recv0.at[2, xx],
                partner,
            )
        )
    stage0.append(remote(vectors, v0, send0.at[3, 0], recv0.at[3, 0], partner))
    for copy in copies + stage0:
        copy.start()
    for copy in stage0:
        copy.wait()
    for xx in range(s.x):
        for zz in range(s.z):
            for yy in range(s.y):
                src = (xx * s.core + core) * block + zz * s.y + yy
                pos = zz * s.y + yy
                to = xx * s.y + yy
                e1[to, zz] = (early[src].astype(F32) + e0[xx, pos].astype(F32)).astype(BF)
                l1[to, zz] = (late[src].astype(F32) + l0[xx, pos].astype(F32)).astype(BF)
                f1[to, pl.ds(zz * units, units)] = (
                    fold[pl.ds(src * units, units), :] + f0[xx, pl.ds(pos * units, units)]
                )
    v1[...] = vectors[...] + v0[...]
    stage1 = []
    for n, (dx, dy) in enumerate(plane):
        to = ((x + dx) % s.x) * s.y + (y + dy) % s.y
        peer = plane_peer(dx, dy)
        for k, (src, dst) in enumerate(((e1, er1), (l1, lr1), (f1, fr1))):
            stage1.append(remote(src.at[to], dst.at[n], send1.at[k, n], recv1.at[k, n], peer))
        stage1.append(remote(v1, vr1.at[n], send1.at[3, n], recv1.at[3, n], peer))
    for copy in stage1:
        copy.start()
    for copy in stage1:
        copy.wait()
    mine = x * s.y + y
    e_sum, l_sum = e1[mine].astype(F32), l1[mine].astype(F32)
    f_sum, v_sum = f1[mine], v1[...]
    for n in range(len(plane)):
        e_sum = e_sum + er1[n].astype(F32)
        l_sum = l_sum + lr1[n].astype(F32)
        f_sum = f_sum + fr1[n]
        v_sum = v_sum + vr1[n]
    e2[...] = e_sum.astype(BF)
    l2[...] = l_sum.astype(BF)
    f2[...] = f_sum
    v2[...] = v_sum
    stage2 = []
    for dz in range(1, s.z):
        to = (z + dz) % s.z
        peer = line_peer(dz)
        n = dz - 1
        stage2.append(remote(e2.at[to], er2.at[n], send2.at[0, n], recv2.at[0, n], peer))
        stage2.append(remote(l2.at[to], lr2.at[n], send2.at[1, n], recv2.at[1, n], peer))
        stage2.append(
            remote(
                f2.at[pl.ds(to * units, units)], fr2.at[n], send2.at[2, n], recv2.at[2, n], peer
            )
        )
        stage2.append(remote(v2, vr2.at[n], send2.at[3, n], recv2.at[3, n], peer))
    for copy in stage2:
        copy.start()
    for copy in copies:
        copy.wait()
    border = onehot(iota((s.node, s.hrows), 0) == out_rows[0:1, :])
    node_grad[...] = node_part[...] + dot(border, back[...])
    for copy in stage2:
        copy.wait()
    e_sum, l_sum = e2[z].astype(F32), l2[z].astype(F32)
    f_sum, v_sum = f2[pl.ds(z * units, units), :], v2[...]
    for n in range(s.z - 1):
        e_sum = e_sum + er2[n].astype(F32)
        l_sum = l_sum + lr2[n].astype(F32)
        f_sum = f_sum + fr2[n]
        v_sum = v_sum + vr2[n]
    early_out[...] = e_sum
    late_out[...] = l_sum
    vec_out[...] = v_sum
    for c in range(COARSE):
        for q in range(cuts):
            j = c * cuts + q
            span = slice(q * LANES, (q + 1) * LANES)
            node_grad[c : c + 1, span] += f_sum[j : j + 1, :]


def reduce_all(s, out_rows, need, node_part, ext_grad, early, late, vectors):
    width = node_part.shape[1]
    units = COARSE * width // LANES
    per_e, per_l = early.shape[1], late.shape[1]
    block = s.z * s.y
    planes = s.x * s.y
    full = pl.BlockSpec(memory_space=VMEM)
    sem = pltpu.SemaphoreType.DMA
    return pl.pallas_call(
        functools.partial(reduce_kernel, s),
        out_shape=[
            jax.ShapeDtypeStruct(node_part.shape, F32),
            jax.ShapeDtypeStruct((per_e, width), F32),
            jax.ShapeDtypeStruct((per_l, width), F32),
            jax.ShapeDtypeStruct(vectors.shape, F32),
        ],
        in_specs=[full] * 7,
        out_specs=[full] * 4,
        scratch_shapes=[
            VMEM((s.dev * units, LANES), F32),
            VMEM((s.hrows, width), BF),
            VMEM((s.x, block, per_e, width), BF),
            VMEM((s.x, block, per_l, width), BF),
            VMEM((s.x, block * units, LANES), F32),
            VMEM(vectors.shape, F32),
            VMEM((planes, s.z, per_e, width), BF),
            VMEM((planes, s.z, per_l, width), BF),
            VMEM((planes, s.z * units, LANES), F32),
            VMEM(vectors.shape, F32),
            VMEM((planes - 1, s.z, per_e, width), BF),
            VMEM((planes - 1, s.z, per_l, width), BF),
            VMEM((planes - 1, s.z * units, LANES), F32),
            VMEM((planes - 1,) + vectors.shape, F32),
            VMEM((s.z, per_e, width), BF),
            VMEM((s.z, per_l, width), BF),
            VMEM((s.z * units, LANES), F32),
            VMEM(vectors.shape, F32),
            VMEM((s.z - 1, per_e, width), BF),
            VMEM((s.z - 1, per_l, width), BF),
            VMEM((s.z - 1, units, LANES), F32),
            VMEM((s.z - 1,) + vectors.shape, F32),
            sem((4,)),
            sem((4,)),
            sem((4, s.x)),
            sem((4, s.x)),
            sem((4, planes - 1)),
            sem((4, planes - 1)),
            sem((4, s.z - 1)),
            sem((4, s.z - 1)),
        ],
        compiler_params=pltpu.CompilerParams(collective_id=1, has_side_effects=True),
        name="reduce",
    )(out_rows, need, node_part, ext_grad, early, late, vectors)


def shards(mesh, nodes, edges, senders, receivers, edge_count, halo_send, long_need, node_cot,
           edge_cot, e_w1, e_b1, e_w2, e_gain, n_w1, n_b1, n_w2, n_gain):
    nodes_l, edges_l = nodes[0, 0], edges[0, 0]
    node_n, width = nodes_l.shape
    edge_n = edges_l.shape[0]
    halo_n, slot_n = halo_send.shape[3], long_need.shape[3]
    s = Sizes(mesh, node_n, halo_n, slot_n)
    rows = jnp.pad(halo_send[0, 0], ((0, 0), (0, s.hslot - halo_n)), constant_values=-1)
    rows = rows.reshape(1, 4 * s.hslot)
    rows = jnp.pad(rows, ((0, 0), (0, s.hrows - 4 * s.hslot)), constant_values=-1)
    need = jnp.pad(
        long_need[0, 0].reshape(1, s.far_n), ((0, 0), (0, s.far - s.far_n)), constant_values=-1
    )
    ext = exchange_table(s, nodes_l, rows, need)
    weights = (e_w1, e_b1[None], e_w2, e_gain[None], n_w1, n_b1[None], n_w2, n_gain[None])
    ids = (edge_n // LANES, LANES)
    new_edges, edge_grad, new_nodes, node_part, ext_grad, early, late, vectors = layer(
        s, edge_count, senders.reshape(ids), receivers.reshape(ids), nodes_l, ext, edges_l,
        edge_cot[0, 0], node_cot[0, 0], weights,
    )
    late = late.reshape(s.dev, -1, width)
    node_grad, e_out, l_out, v_out = reduce_all(
        s, rows, need, node_part, ext_grad, early, late, vectors
    )
    me = lax.axis_index("lat") * s.lon + lax.axis_index("lon")
    part = width // s.dev
    vec = lax.dynamic_slice(v_out[:4], (0, me * part), (4, part))
    one, two = n_w1.shape[0] // s.dev, n_w2.shape[0] // s.dev
    return (
        new_nodes[None, None],
        new_edges[None, None],
        node_grad[None, None],
        edge_grad[None, None],
        l_out,
        vec[0],
        e_out[one + two :],
        vec[1],
        e_out[:one],
        vec[2],
        e_out[one : one + two],
        vec[3],
    )


def solution(mesh):
    grid4, grid3, both = P("lat", "lon", None, None), P("lat", "lon", None), P(("lat", "lon"))
    rows = P(("lat", "lon"), None)
    return jax.shard_map(
        functools.partial(shards, mesh),
        mesh=mesh,
        in_specs=(grid4, grid4, grid3, grid3, P("lat", "lon"), grid4, grid4, grid4, grid4)
        + (P(),) * 8,
        out_specs=(grid4,) * 4 + (rows, both) * 4,
        check_vma=False,
    )
```

time: 194 us -> 116 us (0.60)
  Pallas kernels: 0 us -> 104 us
  waiting for transfers between devices: 53.2 us -> 0 us
  matrix products: 52.9 us -> 0 us
  starting transfers between devices: 35.6 us -> 0 us
  local copies, waits for them, and re-layouts: 35.3 us -> 10.2 us
  other arithmetic: 13.4 us -> 0 us
    pallas_call x0 -> x3, Pallas kernels: none -> 104 us  [the longest x1 46.1 us: reduce_all(): pl.pallas_call(functools.partial(reduce_kernel, s), out_shape=[jax.ShapeD...]
    dot_general x26 -> x0, matrix products: 52.9 us -> none  [the longest x14 42.6 us: product(): return jnp.dot(left, right, preferred_element_type=jnp.float32)]
    all_to_all x4 -> x0, waiting for transfers between devices: 43.8 us -> none  [exchange(): return lax.all_to_all(value, axes, split_axis=0, concat_axis=0, tiled=True)]
    unnamed x99 -> x2, local copies, waits for them, and re-layouts: 29.1 us -> 3.6 us
    all_to_all x4 -> x0, starting transfers between devices: 19 us -> none  [exchange(): return lax.all_to_all(value, axes, split_axis=0, concat_axis=0, tiled=True)]
    ppermute x8 -> x0, starting transfers between devices: 16.6 us -> none  [the longest x4 9.26 us: shifted(): return lax.ppermute(block, axis, route)]
    ppermute x8 -> x0, waiting for transfers between devices: 9.45 us -> none  [the longest x4 9.44 us: shifted(): return lax.ppermute(block, axis, route)]
    convert_element_type x4 -> x0, other arithmetic: 5.02 us -> none  [the longest x1 2.08 us: shards(): g_second = g_second.astype(jnp.bfloat16)]
  transfers between devices with their start and end apart: 12 -> 0, of which waited for: 5 -> 0; matrix products, arithmetic and copies ran while one was open for 26% -> 0% of each run, Pallas kernels for 0% -> 0%
where the time goes in v1:
time: 116 us; the launch traced here: 115 us
  Pallas kernels  104 us (90%)
  local copies, waits for them, and re-layouts  10.2 us (9%)
  between operations  1.32 us (1%)
    pallas_call x1, Pallas kernels, reduce_all(): pl.pallas_call(functools.partial(reduce_kernel, s), out_shape=[jax.ShapeD...  46.1 us
    pallas_call x1, Pallas kernels, layer(): pl.pallas_call(functools.partial(layer_kernel, s), grid=(2 * steps,), out...  43.1 us
    pallas_call x1, Pallas kernels, exchange_table(): pl.pallas_call(functools.partial(table_kernel, s), out_shape=jax.ShapeDty...  14.7 us
    unnamed x2, local copies, waits for them, and re-layouts  3.6 us

profile of v1, /device:TPU:0, one launch (start us, length us, event | category | flops | bytes accessed | tf_op | source)
XLA Modules:
  0.0 115.4 jit_solution(6698952021135566501)
XLA Ops:
  0.6 0.7 pad.8
  1.3 0.6 reshape.38.out_rows
  1.9 1.2 %pad.9.need = s32[1,128]{1,0:T(1,128)} pad(s32[1,32]{1,0:T(1,128)} %bitcast.42, s32[]{:T(128)} %constant.7.clone.1), padding=0_0x0_96 | pad | bytes 644 | tf_op jit(solution)/shard_map/jit(_pad)/pad | solution.py:670
  3.1 14.7 %table.1.ext = bf16[256,512]{1,0:T(8,128)(2,1)} custom-call(bf16[384,512]{1,0:T(8,128)(2,1)} %bitcast.27, s32[1,128]{1,0:T(1,128)} %reshape.38.out_rows, s32[1,128]{1,0:T(1,128)} %pad.9.need), custom_call_target="tpu_custom_call" | custom-call | tf_op jit(solution)/shard_map/table/pallas_call | solution.py:163
  18.4 43.1 %layer.1 = (bf16[3072,512]{1,0:T(8,128)(2,1)}, f32[3072,512]{1,0:T(8,128)}, bf16[384,512]{1,0:T(8,128)(2,1)}, f32[384,512]{1,0:T(8,128)}, bf16[256,512]{1,0:T(8,...) custom-call(s32[1,1]{1,0:T(1,128)S(6)} %copy.31.count, s32[24,128]{1,0:T(8,128)} %bitcast.32, ...), custom_call_target="tpu_custom_call" | custom-call | tf_op jit(solution)/shard_map/layer/pallas_call | solution.py:400
  61.5 46.1 %reduce.1 = (f32[384,512]{1,0:T(8,128)}, f32[64,512]{1,0:T(8,128)}, f32[48,512]{1,0:T(8,128)}, f32[8,512]{1,0:T(8,128)}) custom-call(s32[1,128]{1,0:T(1,128)} %reshape.38.out_rows, s32[1,128]{1,0:T(1,128)} %pad.9.need, f32[384,512]{1,0:T(8,128)} %get-tuple-element.26.node_part, bf16[256,512]{1,0:T(8,128)(2,1)} %get-tuple-element.27.ext_grad, ...), custom_call_target="tpu_custom_call" | custom-call | tf_op jit(solution)/shard_map/reduce/pallas_call | solution.py:613
  107.6 0.7 slice.24
  108.3 0.1 constant_dynamic-slice_fusion
  108.4 0.5 slice_bitcast_fusion
  108.9 1.4 %fusion = (f32[16,512]{1,0:T(8,128)}, f32[16,512]{1,0:T(8,128)}) fusion(f32[64,512]{1,0:T(8,128)} %get-tuple-element.35), kind=kLoop, calls=%fused_computation.5 | loop fusion | bytes 131072 | tf_op jit(solution)/shard_map/slice | solution.py:699
  110.3 1.5 %slice.28 = f32[32,512]{1,0:T(8,128)} slice(f32[64,512]{1,0:T(8,128)} %get-tuple-element.35), slice={[0:32], [0:512]} | slice | bytes 131072 | tf_op jit(solution)/shard_map/slice | solution.py:697
  111.8 2.1 %copy.32 = f32[1,1,384,512]{3,2,1,0:T(8,128)} copy(f32[1,1,384,512]{3,2,1,0:T(8,128)} %bitcast.30) | data formatting | bytes 1572864
  113.8 1.5 %copy.33 = f32[48,512]{1,0:T(8,128)} copy(f32[48,512]{1,0:T(8,128)} %get-tuple-element.58) | data formatting | bytes 196608
